TPU v7x, 8 devices: a whole 2x2x1 slice. The times are simulated.
8 devices in a mesh: rep: 1 (over z), dp: 8 (over x, y, core).
Axes of the slice: x: 2, y: 2, z: 1, core: 2. Of those that a mesh axis runs over, the one named last changes fastest.
Arguments:
- a: bfloat16 [8, 4, 4096, 1024], P(('rep', 'dp'))
- g: bfloat16 [8, 4, 4096, 3200], P(('rep', 'dp'))
Outputs:
- output: bfloat16 [4, 1024, 3200], P('rep')
All inputs are finite; a program needn't handle non-finite values.
Results may differ from a plain program's by a relative error of at most 0.012.
Values are sent between devices in bfloat16 or wider.
A program may use at most 2 GiB of HBM per device.

v0:
```python
import jax
import jax.numpy as jnp


def solution(mesh):
    groups = mesh.shape["rep"]

    def step(a, g):
        a, g = (t.reshape(groups, -1, *t.shape[1:]) for t in (a, g))
        sums = jnp.einsum("rsntd,rsntf->rndf", a, g, preferred_element_type=jnp.float32)
        return sums.astype(jnp.bfloat16).reshape(-1, *sums.shape[2:])

    return step
```

profile of v0, /device:TPU:0, one launch (start us, length us, event | category | flops | bytes accessed | tf_op | source)
XLA Modules:
  0.0 738.4 jit_solution(11993047079878110040)
XLA Ops:
  0.0 128.3 %fusion = f32[4,1024,3200]{2,1,0:T(8,128)} fusion(bf16[1,4,4096,3200]{3,2,1,0:T(8,128)(2,1)} %param.1, bf16[1,4,4096,1024]{3,2,1,0:T(8,128)(2,1)} %param), kind=kOutput, calls=%fused_computation | convolution fusion | flops 107374182400 | bytes 190840832 | tf_op jit(solution)/rsntd,rsntf->rndf/dot_general | solution.py:10
  128.3 610.1 %all-reduce.2 = bf16[4,1024,3200]{2,1,0:T(8,128)(2,1)} all-reduce(f32[4,1024,3200]{2,1,0:T(8,128)} %fusion), channel_id=1, replica_groups=mesh['axis_0'=8] {'axis_0'}, use_global_device_ids=true, to_apply=%add.clone | all-reduce | flops 13107200 | bytes 78643200 | tf_op jit(solution)/rsntd,rsntf->rndf/dot_general | solution.py:10
where the time goes:
time: 739 us; the launch traced here: 738 us
  blocking collectives  610 us (83%)
  matrix products  128 us (17%)
    dot_general x1, blocking collectives, step(): jnp.einsum('rsntd,rsntf->rndf', a, g, preferred_element_type=jnp.float32)  610 us
    dot_general x1, matrix products, step(): jnp.einsum('rsntd,rsntf->rndf', a, g, preferred_element_type=jnp.float32)  128 us

commit v1 on v0

v1 whole, which is shorter than its diff:
```python
import functools

import jax
import jax.numpy as jnp
from jax import lax
from jax.experimental import pallas as pl
from jax.experimental.pallas import tpu as pltpu
from jax.sharding import PartitionSpec as P

MESH = pl.DeviceIdType.MESH
ROWS, COLS = 512, 640
RING = 4
GATHER_FROM, GATHER_EVERY = 4, 2


def kernel(dims, a, g, out, a_v, g_v, half_send, half_own, half_recv, one_send, one_own, one_recv, two_send, two_own,
           two_recv, final, sem_a, sem_g, sem_hs, sem_hr, sem_1s, sem_1r, sem_2s, sem_2r, sem_fin, sem_3s, sem_3r,
           sem_4s, sem_4r, sem_5s, sem_5r, sem_6s, sem_6r):
    mats, tokens, d, ff = dims
    row_blocks, col_blocks = d // ROWS, ff // COLS
    steps = mats * row_blocks * col_blocks
    half, quarter, eighth = ROWS // 2, ROWS // 4, ROWS // 8

    me = lax.axis_index("dp")
    core, y, x = me % 2, (me // 2) % 2, me // 4
    mate = me + 1 - 2 * core
    first_bit = x * (1 - core) + y * core
    second_bit = y * (1 - core) + x * core
    first = me + (1 - 2 * first_bit) * (4 - 2 * core)
    second = me + (1 - 2 * second_bit) * (2 + 2 * core)

    def send(src, dst, send_sem, recv_sem, to):
        return pltpu.make_async_remote_copy(src, dst, send_sem, recv_sem, device_id={"dp": to}, device_id_type=MESH)

    barrier = pltpu.get_barrier_semaphore()
    for to in (mate, first, second):
        pl.semaphore_signal(barrier, 1, device_id={"dp": to}, device_id_type=MESH)

    def place(k):
        n = k // (row_blocks * col_blocks)
        rest = k % (row_blocks * col_blocks)
        return n, rest // row_blocks, rest % row_blocks

    def load_a(n, r):
        cols = pl.ds(pl.multiple_of(r * ROWS, ROWS), ROWS)
        return pltpu.make_async_copy(a.at[0, n, :, cols], a_v.at[n % 2, :, cols], sem_a.at[n % 2, r])

    def load_g(i):
        n, c = i // col_blocks, i % col_blocks
        cols = pl.ds(pl.multiple_of(c * COLS, 128), COLS)
        return pltpu.make_async_copy(g.at[0, n, :, cols], g_v.at[i % 2], sem_g.at[i % 2])

    def rows_of(k, start, size):
        n, c, r = place(k)
        return out.at[n, pl.ds(pl.multiple_of(r * ROWS + start, eighth), size), pl.ds(pl.multiple_of(c * COLS, 128), COLS)]

    own_half = core * half
    here = own_half + first_bit * quarter + second_bit * eighth
    there = own_half + first_bit * quarter + (1 - second_bit) * eighth

    def swap(k):
        return send(half_send.at[k % 2], half_recv.at[k], sem_hs.at[k % 2], sem_hr.at[k], mate)

    def exchange_one(k):
        return send(one_send.at[k % RING], one_recv.at[k], sem_1s.at[k % RING], sem_1r.at[k], first)

    def exchange_two(k):
        return send(two_send.at[k % RING], two_recv.at[k], sem_2s.at[k % RING], sem_2r.at[k], second)

    def keep(k):
        return pltpu.make_async_copy(final.at[k], rows_of(k, here, eighth), sem_fin.at[k])

    def gather_second(k):
        return send(final.at[k], rows_of(k, here, eighth), sem_3s.at[k], sem_3r.at[k], second)

    def gather_first(k):
        return send(final.at[k], rows_of(k, here, eighth), sem_4s.at[k], sem_4r.at[k], first)

    def relay(k):
        return send(rows_of(k, there, eighth), rows_of(k, there, eighth), sem_5s.at[k], sem_5r.at[k], first)

    def hand_over(k):
        return send(rows_of(k, own_half, half), rows_of(k, own_half, half), sem_6s.at[k], sem_6r.at[k], mate)

    def product(k, start):
        n, c, r = place(k)
        cols = pl.ds(pl.multiple_of(r * ROWS + start, half), half)
        return lax.dot_general(
            a_v[n % 2, :, cols], g_v[(k // row_blocks) % 2], (((0,), (0,)), ((), ())), preferred_element_type=jnp.float32
        )

    def part(ref, slot, bit, size):
        return ref[slot, pl.ds(pl.multiple_of(bit * size, size), size), :]

    def reduce_cores(k):
        swap(k).wait_recv()

        @pl.when(k >= RING)
        def _():
            exchange_one(k - RING).wait_send()

        def total(bit):
            return part(half_own, k % 2, bit, quarter) + part(half_recv, k, bit, quarter).astype(jnp.float32)

        one_send[k % RING] = total(1 - first_bit).astype(jnp.bfloat16)
        one_own[k % 2] = total(first_bit)
        exchange_one(k).start()

    def reduce_first(k):
        exchange_one(k).wait_recv()

        @pl.when(k >= RING)
        def _():
            exchange_two(k - RING).wait_send()

        def total(bit):
            return part(one_own, k % 2, bit, eighth) + part(one_recv, k, bit, eighth).astype(jnp.float32)

        two_send[k % RING] = total(1 - second_bit).astype(jnp.bfloat16)
        two_own[k % 2] = total(second_bit)
        exchange_two(k).start()

    def reduce_second(k):
        exchange_two(k).wait_recv()
        final[k] = (two_own[k % 2] + two_recv[k].astype(jnp.float32)).astype(jnp.bfloat16)
        keep(k).start()

    def gather(k):
        gather_second(k).start()
        gather_first(k).start()

    def pass_on(k):
        gather_second(k).wait_recv()
        relay(k).start()

    def finish(k):
        keep(k).wait()
        gather_first(k).wait_recv()
        relay(k).wait_recv()
        hand_over(k).start()

    load_a(0, 0).start()
    load_g(0).start()
    for r in range(1, row_blocks):
        load_a(0, r).start()
    pl.semaphore_wait(barrier, 3)

    def step(k, carry):
        n, c, r = place(k)

        @pl.when(r == 0)
        def _():
            load_g(k // row_blocks).wait()

            @pl.when(k + row_blocks < steps)
            def _():
                load_g(k // row_blocks + 1).start()

        @pl.when(c == 0)
        def _():
            load_a(n, r).wait()

            @pl.when(n + 1 < mats)
            def _():
                load_a(n + 1, r).start()

        @pl.when(k >= 2)
        def _():
            swap(k - 2).wait_send()

        half_send[k % 2] = product(k, (1 - core) * half).astype(jnp.bfloat16)
        swap(k).start()
        half_own[k % 2] = product(k, own_half)
        reduce_cores(k)

        @pl.when(k >= 1)
        def _():
            reduce_first(k - 1)

        @pl.when(k >= 2)
        def _():
            reduce_second(k - 2)

        @pl.when((k >= GATHER_FROM) & ((k - GATHER_FROM) % GATHER_EVERY == 0))
        def _():
            i = (k - GATHER_FROM) // GATHER_EVERY
            gather(i)

            @pl.when(i >= 2)
            def _():
                pass_on(i - 2)

            @pl.when(i >= 4)
            def _():
                finish(i - 4)

        return carry

    lax.fori_loop(0, steps, step, 0)
    reduce_first(steps - 1)
    reduce_second(steps - 2)
    reduce_second(steps - 1)

    started = (steps - 1 - GATHER_FROM) // GATHER_EVERY + 1

    def loop(low, high, f):
        def body(k, carry):
            f(k)
            return carry

        lax.fori_loop(low, high, body, 0)

    loop(started, steps, gather)
    loop(started - 2, steps, pass_on)
    loop(started - 4, steps, finish)

    def drain(k):
        gather_second(k).wait_send()
        gather_first(k).wait_send()
        relay(k).wait_send()
        hand_over(k).wait()

    loop(0, steps, drain)
    for k in range(steps - 2, steps):
        swap(k).wait_send()
    for k in range(steps - RING, steps):
        exchange_one(k).wait_send()
        exchange_two(k).wait_send()


def solution(mesh):
    def step(a, g):
        _, mats, tokens, d = a.shape
        ff = g.shape[-1]
        steps = mats * (d // ROWS) * (ff // COLS)
        half, quarter, eighth = ROWS // 2, ROWS // 4, ROWS // 8
        bf16, f32 = jnp.bfloat16, jnp.float32
        dma = pltpu.SemaphoreType.DMA
        return pl.pallas_call(
            functools.partial(kernel, (mats, tokens, d, ff)),
            out_shape=jax.ShapeDtypeStruct((mats, d, ff), bf16),
            in_specs=[pl.BlockSpec(memory_space=pl.ANY)] * 2,
            out_specs=pl.BlockSpec(memory_space=pl.ANY),
            scratch_shapes=[
                pltpu.VMEM((2, tokens, d), bf16),
                pltpu.VMEM((2, tokens, COLS), bf16),
                pltpu.VMEM((2, half, COLS), bf16),
                pltpu.VMEM((2, half, COLS), f32),
                pltpu.VMEM((steps, half, COLS), bf16),
                pltpu.VMEM((RING, quarter, COLS), bf16),
                pltpu.VMEM((2, quarter, COLS), f32),
                pltpu.VMEM((steps, quarter, COLS), bf16),
                pltpu.VMEM((RING, eighth, COLS), bf16),
                pltpu.VMEM((2, eighth, COLS), f32),
                pltpu.VMEM((steps, eighth, COLS), bf16),
                pltpu.VMEM((steps, eighth, COLS), bf16),
                dma((2, d // ROWS)),
                dma((2,)),
                dma((2,)),
                dma((steps,)),
                dma((RING,)),
                dma((steps,)),
                dma((RING,)),
                dma((steps,)),
            ]
            + [dma((steps,))] * 9,
            compiler_params=pltpu.CompilerParams(
                collective_id=0, has_side_effects=True, vmem_limit_bytes=63 * 2**20
            ),
        )(a, g)

    return jax.shard_map(
        step,
        mesh=mesh,
        in_specs=(P(("rep", "dp")), P(("rep", "dp"))),
        out_specs=P("rep"),
        check_vma=False,
    )
```

time: 739 us -> 285 us (0.39)
  blocking collectives: 610 us -> 0 us
  Pallas kernels: 0 us -> 267 us
  matrix products: 128 us -> 0 us
  local copies, waits for them, and re-layouts: 0 us -> 18 us
    dot_general x1 -> x0, blocking collectives: 610 us -> none  [step(): jnp.einsum('rsntd,rsntf->rndf', a, g, preferred_element_type=jnp.float32)]
    pallas_call x0 -> x1, Pallas kernels: none -> 267 us  [step(): pl.pallas_call(functools.partial(kernel, (mats, tokens, d, ff)), out_shap...]
    dot_general x1 -> x0, matrix products: 128 us -> none  [step(): jnp.einsum('rsntd,rsntf->rndf', a, g, preferred_element_type=jnp.float32)]
    unnamed x0 -> x1, local copies, waits for them, and re-layouts: none -> 18 us
where the time goes in v1:
time: 285 us
  Pallas kernels  267 us (94%)
  local copies, waits for them, and re-layouts  18 us (6%)
    pallas_call x1, Pallas kernels, step(): pl.pallas_call(functools.partial(kernel, (mats, tokens, d, ff)), out_shap...  267 us
    unnamed x1, local copies, waits for them, and re-layouts  18 us

profile of v1, /device:TPU:0, one launch (start us, length us, event | category | flops | bytes accessed | tf_op | source)
XLA Modules:
  0.0 285.1 jit_solution(9686377340037589536)
XLA Ops:
  0.0 267.1 %shard_map.28 = bf16[4,1024,3200]{2,1,0:T(8,128)(2,1)} custom-call(bf16[1,4,4096,1024]{3,2,1,0:T(8,128)(2,1)} %a.1, bf16[1,4,4096,3200]{3,2,1,0:T(8,128)(2,1)} %g.1), custom_call_target="tpu_custom_call" | custom-call | tf_op jit(solution)/shard_map/pallas_call | solution.py:239
  267.1 18.0 %copy.4 = bf16[4,1024,3200]{2,1,0:T(8,128)(2,1)} copy(bf16[4,1024,3200]{2,1,0:T(8,128)(2,1)} %shard_map.28) | data formatting | bytes 52428800

commit v2 on v1

--- a/solution.py
+++ b/solution.py
@@ -9,8 +9,13 @@
 
 MESH = pl.DeviceIdType.MESH
 ROWS, COLS = 512, 640
-RING = 4
-GATHER_FROM, GATHER_EVERY = 4, 2
+VMEM_LIMIT = 63 * 2**20
+LAG_ONE, LAG_TWO = 2, 4
+RING_ONE, RING_TWO = 2 * LAG_ONE + 2, 2 * (LAG_TWO - LAG_ONE) + 2
+OWN_ONE, OWN_TWO = LAG_ONE + 1, LAG_TWO - LAG_ONE + 1
+GATHER_FROM, GATHER_SKIP = LAG_TWO, 6
+PASS_LAG, FINISH_LAG = 2, 4
+TAIL = 2
 
 
 def kernel(dims, a, g, out, a_v, g_v, half_send, half_own, half_recv, one_send, one_own, one_recv, two_send, two_own,
@@ -50,22 +55,25 @@
         cols = pl.ds(pl.multiple_of(c * COLS, 128), COLS)
         return pltpu.make_async_copy(g.at[0, n, :, cols], g_v.at[i % 2], sem_g.at[i % 2])
 
+    def index(k, start, size):
+        n, c, r = place(k)
+        return n, pl.ds(pl.multiple_of(r * ROWS + start, eighth), size), pl.ds(pl.multiple_of(c * COLS, 128), COLS)
+
     def rows_of(k, start, size):
-        n, c, r = place(k)
-        return out.at[n, pl.ds(pl.multiple_of(r * ROWS + start, eighth), size), pl.ds(pl.multiple_of(c * COLS, 128), COLS)]
+        return out.at[index(k, start, size)]
 
     own_half = core * half
     here = own_half + first_bit * quarter + second_bit * eighth
     there = own_half + first_bit * quarter + (1 - second_bit) * eighth
 
     def swap(k):
-        return send(half_send.at[k % 2], half_recv.at[k], sem_hs.at[k % 2], sem_hr.at[k], mate)
+        return send(half_send.at[k % 2], half_recv.at[k % 2], sem_hs.at[k % 2], sem_hr.at[k % 2], mate)
 
     def exchange_one(k):
-        return send(one_send.at[k % RING], one_recv.at[k], sem_1s.at[k % RING], sem_1r.at[k], first)
+        return send(one_send.at[k % RING_ONE], one_recv.at[k % RING_ONE], sem_1s.at[k % RING_ONE], sem_1r.at[k % RING_ONE], first)
 
     def exchange_two(k):
-        return send(two_send.at[k % RING], two_recv.at[k], sem_2s.at[k % RING], sem_2r.at[k], second)
+        return send(two_send.at[k % RING_TWO], two_recv.at[k % RING_TWO], sem_2s.at[k % RING_TWO], sem_2r.at[k % RING_TWO], second)
 
     def keep(k):
         return pltpu.make_async_copy(final.at[k], rows_of(k, here, eighth), sem_fin.at[k])
@@ -95,34 +103,34 @@
     def reduce_cores(k):
         swap(k).wait_recv()
 
-        @pl.when(k >= RING)
-        def _():
-            exchange_one(k - RING).wait_send()
+        @pl.when(k >= RING_ONE)
+        def _():
+            exchange_one(k - RING_ONE).wait_send()
 
         def total(bit):
-            return part(half_own, k % 2, bit, quarter) + part(half_recv, k, bit, quarter).astype(jnp.float32)
-
-        one_send[k % RING] = total(1 - first_bit).astype(jnp.bfloat16)
-        one_own[k % 2] = total(first_bit)
+            return part(half_own, k % 2, bit, quarter) + part(half_recv, k % 2, bit, quarter).astype(jnp.float32)
+
+        one_send[k % RING_ONE] = total(1 - first_bit).astype(jnp.bfloat16)
+        one_own[k % OWN_ONE] = total(first_bit)
         exchange_one(k).start()
 
     def reduce_first(k):
         exchange_one(k).wait_recv()
 
-        @pl.when(k >= RING)
-        def _():
-            exchange_two(k - RING).wait_send()
+        @pl.when(k >= RING_TWO)
+        def _():
+            exchange_two(k - RING_TWO).wait_send()
 
         def total(bit):
-            return part(one_own, k % 2, bit, eighth) + part(one_recv, k, bit, eighth).astype(jnp.float32)
-
-        two_send[k % RING] = total(1 - second_bit).astype(jnp.bfloat16)
-        two_own[k % 2] = total(second_bit)
+            return part(one_own, k % OWN_ONE, bit, eighth) + part(one_recv, k % RING_ONE, bit, eighth).astype(jnp.float32)
+
+        two_send[k % RING_TWO] = total(1 - second_bit).astype(jnp.bfloat16)
+        two_own[k % OWN_TWO] = total(second_bit)
         exchange_two(k).start()
 
     def reduce_second(k):
         exchange_two(k).wait_recv()
-        final[k] = (two_own[k % 2] + two_recv[k].astype(jnp.float32)).astype(jnp.bfloat16)
+        final[k] = (two_own[k % OWN_TWO] + two_recv[k % RING_TWO].astype(jnp.float32)).astype(jnp.bfloat16)
         keep(k).start()
 
     def gather(k):
@@ -173,35 +181,34 @@
         half_own[k % 2] = product(k, own_half)
         reduce_cores(k)
 
-        @pl.when(k >= 1)
-        def _():
-            reduce_first(k - 1)
-
-        @pl.when(k >= 2)
-        def _():
-            reduce_second(k - 2)
-
-        @pl.when((k >= GATHER_FROM) & ((k - GATHER_FROM) % GATHER_EVERY == 0))
-        def _():
-            i = (k - GATHER_FROM) // GATHER_EVERY
+        @pl.when(k >= LAG_ONE)
+        def _():
+            reduce_first(k - LAG_ONE)
+
+        @pl.when(k >= LAG_TWO)
+        def _():
+            reduce_second(k - LAG_TWO)
+
+        since = k - GATHER_FROM
+
+        @pl.when((since >= 0) & (since % GATHER_SKIP != GATHER_SKIP - 1))
+        def _():
+            i = since - since // GATHER_SKIP
             gather(i)
 
-            @pl.when(i >= 2)
-            def _():
-                pass_on(i - 2)
-
-            @pl.when(i >= 4)
-            def _():
-                finish(i - 4)
+            @pl.when(i >= PASS_LAG)
+            def _():
+                pass_on(i - PASS_LAG)
+
+            @pl.when(i >= FINISH_LAG)
+            def _():
+                finish(i - FINISH_LAG)
 
         return carry
 
     lax.fori_loop(0, steps, step, 0)
-    reduce_first(steps - 1)
-    reduce_second(steps - 2)
-    reduce_second(steps - 1)
-
-    started = (steps - 1 - GATHER_FROM) // GATHER_EVERY + 1
+    since = steps - GATHER_FROM
+    started = since - since // GATHER_SKIP
 
     def loop(low, high, f):
         def body(k, carry):
@@ -210,9 +217,15 @@
 
         lax.fori_loop(low, high, body, 0)
 
-    loop(started, steps, gather)
-    loop(started - 2, steps, pass_on)
-    loop(started - 4, steps, finish)
+    for k in range(steps, steps + LAG_TWO):
+        if k - LAG_ONE < steps:
+            reduce_first(k - LAG_ONE)
+        reduce_second(k - LAG_TWO)
+        ready = min(started + TAIL, k - LAG_TWO + 1) if k + 1 < steps + LAG_TWO else steps
+        loop(started, ready, gather)
+        started = max(started, ready)
+    loop(since - since // GATHER_SKIP - PASS_LAG, steps, pass_on)
+    loop(since - since // GATHER_SKIP - FINISH_LAG, steps, finish)
 
     def drain(k):
         gather_second(k).wait_send()
@@ -223,8 +236,9 @@
     loop(0, steps, drain)
     for k in range(steps - 2, steps):
         swap(k).wait_send()
-    for k in range(steps - RING, steps):
+    for k in range(steps - RING_ONE, steps):
         exchange_one(k).wait_send()
+    for k in range(steps - RING_TWO, steps):
         exchange_two(k).wait_send()
 
 
@@ -246,26 +260,26 @@
                 pltpu.VMEM((2, tokens, COLS), bf16),
                 pltpu.VMEM((2, half, COLS), bf16),
                 pltpu.VMEM((2, half, COLS), f32),
-                pltpu.VMEM((steps, half, COLS), bf16),
-                pltpu.VMEM((RING, quarter, COLS), bf16),
-                pltpu.VMEM((2, quarter, COLS), f32),
-                pltpu.VMEM((steps, quarter, COLS), bf16),
-                pltpu.VMEM((RING, eighth, COLS), bf16),
-                pltpu.VMEM((2, eighth, COLS), f32),
-                pltpu.VMEM((steps, eighth, COLS), bf16),
+                pltpu.VMEM((2, half, COLS), bf16),
+                pltpu.VMEM((RING_ONE, quarter, COLS), bf16),
+                pltpu.VMEM((OWN_ONE, quarter, COLS), f32),
+                pltpu.VMEM((RING_ONE, quarter, COLS), bf16),
+                pltpu.VMEM((RING_TWO, eighth, COLS), bf16),
+                pltpu.VMEM((OWN_TWO, eighth, COLS), f32),
+                pltpu.VMEM((RING_TWO, eighth, COLS), bf16),
                 pltpu.VMEM((steps, eighth, COLS), bf16),
                 dma((2, d // ROWS)),
                 dma((2,)),
                 dma((2,)),
-                dma((steps,)),
-                dma((RING,)),
-                dma((steps,)),
-                dma((RING,)),
-                dma((steps,)),
+                dma((2,)),
+                dma((RING_ONE,)),
+                dma((RING_ONE,)),
+                dma((RING_TWO,)),
+                dma((RING_TWO,)),
             ]
             + [dma((steps,))] * 9,
             compiler_params=pltpu.CompilerParams(
-                collective_id=0, has_side_effects=True, vmem_limit_bytes=63 * 2**20
+                collective_id=0, has_side_effects=True, vmem_limit_bytes=VMEM_LIMIT
             ),
         )(a, g)
 

time: 285 us -> 252 us (0.88)
  Pallas kernels: 267 us -> 234 us
    pallas_call x1, Pallas kernels: 267 us -> 234 us  [step(): pl.pallas_call(functools.partial(kernel, (mats, tokens, d, ff)), out_shap...]
where the time goes in v2:
time: 252 us
  Pallas kernels  234 us (93%)
  local copies, waits for them, and re-layouts  18 us (7%)
    pallas_call x1, Pallas kernels, step(): pl.pallas_call(functools.partial(kernel, (mats, tokens, d, ff)), out_shap...  234 us
    unnamed x1, local copies, waits for them, and re-layouts  18 us

profile of v2, /device:TPU:0, one launch (start us, length us, event | category | flops | bytes accessed | tf_op | source)
XLA Modules:
  0.0 252.1 jit_solution(7975835270437908866)
XLA Ops:
  0.0 234.1 %shard_map.28 = bf16[4,1024,3200]{2,1,0:T(8,128)(2,1)} custom-call(bf16[1,4,4096,1024]{3,2,1,0:T(8,128)(2,1)} %a.1, bf16[1,4,4096,3200]{3,2,1,0:T(8,128)(2,1)} %g.1), custom_call_target="tpu_custom_call" | custom-call | tf_op jit(solution)/shard_map/pallas_call | solution.py:253
  234.1 18.0 %copy.4 = bf16[4,1024,3200]{2,1,0:T(8,128)(2,1)} copy(bf16[4,1024,3200]{2,1,0:T(8,128)(2,1)} %shard_map.28) | data formatting | bytes 52428800

commit v3 on v2

--- a/solution.py
+++ b/solution.py
@@ -15,22 +15,41 @@
 OWN_ONE, OWN_TWO = LAG_ONE + 1, LAG_TWO - LAG_ONE + 1
 GATHER_FROM, GATHER_SKIP = LAG_TWO, 6
 PASS_LAG, FINISH_LAG = 2, 4
+AFTER = 20
+COPY_ROWS, COPY_SLOTS = 256, 6
+
 TAIL = 2
 
 
-def kernel(dims, a, g, out, a_v, g_v, half_send, half_own, half_recv, one_send, one_own, one_recv, two_send, two_own,
+def position(me):
+    core, y, x = me % 2, (me // 2) % 2, me // 4
+    return core, x * (1 - core) + y * core, y * (1 - core) + x * core
+
+
+def place(dims, k):
+    mats, tokens, d, ff = dims
+    row_blocks, col_blocks = d // ROWS, ff // COLS
+    rest = k % (row_blocks * col_blocks)
+    return k // (row_blocks * col_blocks), rest // row_blocks, rest % row_blocks
+
+
+def index(dims, k, start, size):
+    n, c, r = place(dims, k)
+    return n, pl.ds(pl.multiple_of(r * ROWS + start, size), size), pl.ds(pl.multiple_of(c * COLS, 128), COLS)
+
+
+def kernel(dims, a, g, out, later, a_v, g_v, half_send, half_own, half_recv, one_send, one_own, one_recv, two_send, two_own,
            two_recv, final, sem_a, sem_g, sem_hs, sem_hr, sem_1s, sem_1r, sem_2s, sem_2r, sem_fin, sem_3s, sem_3r,
-           sem_4s, sem_4r, sem_5s, sem_5r, sem_6s, sem_6r):
+           sem_4s, sem_4r, sem_5s, sem_5r, sem_6s, sem_6r, sem_7s, sem_7r):
     mats, tokens, d, ff = dims
     row_blocks, col_blocks = d // ROWS, ff // COLS
     steps = mats * row_blocks * col_blocks
     half, quarter, eighth = ROWS // 2, ROWS // 4, ROWS // 8
+    after = steps - AFTER
 
     me = lax.axis_index("dp")
-    core, y, x = me % 2, (me // 2) % 2, me // 4
+    core, first_bit, second_bit = position(me)
     mate = me + 1 - 2 * core
-    first_bit = x * (1 - core) + y * core
-    second_bit = y * (1 - core) + x * core
     first = me + (1 - 2 * first_bit) * (4 - 2 * core)
     second = me + (1 - 2 * second_bit) * (2 + 2 * core)
 
@@ -40,11 +59,6 @@
     barrier = pltpu.get_barrier_semaphore()
     for to in (mate, first, second):
         pl.semaphore_signal(barrier, 1, device_id={"dp": to}, device_id_type=MESH)
-
-    def place(k):
-        n = k // (row_blocks * col_blocks)
-        rest = k % (row_blocks * col_blocks)
-        return n, rest // row_blocks, rest % row_blocks
 
     def load_a(n, r):
         cols = pl.ds(pl.multiple_of(r * ROWS, ROWS), ROWS)
@@ -55,16 +69,13 @@
         cols = pl.ds(pl.multiple_of(c * COLS, 128), COLS)
         return pltpu.make_async_copy(g.at[0, n, :, cols], g_v.at[i % 2], sem_g.at[i % 2])
 
-    def index(k, start, size):
-        n, c, r = place(k)
-        return n, pl.ds(pl.multiple_of(r * ROWS + start, eighth), size), pl.ds(pl.multiple_of(c * COLS, 128), COLS)
-
     def rows_of(k, start, size):
-        return out.at[index(k, start, size)]
+        return out.at[index(dims, k, start, size)]
 
     own_half = core * half
     here = own_half + first_bit * quarter + second_bit * eighth
     there = own_half + first_bit * quarter + (1 - second_bit) * eighth
+    across = own_half + (1 - first_bit) * quarter + second_bit * eighth
 
     def swap(k):
         return send(half_send.at[k % 2], half_recv.at[k % 2], sem_hs.at[k % 2], sem_hr.at[k % 2], mate)
@@ -81,6 +92,9 @@
     def gather_second(k):
         return send(final.at[k], rows_of(k, here, eighth), sem_3s.at[k], sem_3r.at[k], second)
 
+    def gather_later(k):
+        return send(final.at[k], later.at[k - after], sem_3s.at[k], sem_3r.at[k], second)
+
     def gather_first(k):
         return send(final.at[k], rows_of(k, here, eighth), sem_4s.at[k], sem_4r.at[k], first)
 
@@ -90,8 +104,17 @@
     def hand_over(k):
         return send(rows_of(k, own_half, half), rows_of(k, own_half, half), sem_6s.at[k], sem_6r.at[k], mate)
 
+    def hand_over_own(k):
+        return send(final.at[k], rows_of(k, here, eighth), sem_6s.at[k], sem_6r.at[k], mate)
+
+    def hand_over_later(k):
+        return send(later.at[k - after], rows_of(k, there, eighth), sem_5s.at[k], sem_5r.at[k], mate)
+
+    def hand_over_across(k):
+        return send(rows_of(k, across, eighth), rows_of(k, across, eighth), sem_7s.at[k - after], sem_7r.at[k - after], mate)
+
     def product(k, start):
-        n, c, r = place(k)
+        n, c, r = place(dims, k)
         cols = pl.ds(pl.multiple_of(r * ROWS + start, half), half)
         return lax.dot_general(
             a_v[n % 2, :, cols], g_v[(k // row_blocks) % 2], (((0,), (0,)), ((), ())), preferred_element_type=jnp.float32
@@ -133,19 +156,44 @@
         final[k] = (two_own[k % OWN_TWO] + two_recv[k % RING_TWO].astype(jnp.float32)).astype(jnp.bfloat16)
         keep(k).start()
 
+    def either(k, before, tail):
+        pl.when(k < after)(before)
+        pl.when(k >= after)(tail)
+
     def gather(k):
-        gather_second(k).start()
+        def before():
+            gather_second(k).start()
+
+        def tail():
+            gather_later(k).start()
+            hand_over_own(k).start()
+
+        either(k, before, tail)
         gather_first(k).start()
 
     def pass_on(k):
-        gather_second(k).wait_recv()
-        relay(k).start()
+        def before():
+            gather_second(k).wait_recv()
+            relay(k).start()
+
+        def tail():
+            gather_later(k).wait_recv()
+            hand_over_later(k).start()
+
+        either(k, before, tail)
 
     def finish(k):
         keep(k).wait()
         gather_first(k).wait_recv()
-        relay(k).wait_recv()
-        hand_over(k).start()
+
+        def before():
+            relay(k).wait_recv()
+            hand_over(k).start()
+
+        def tail():
+            hand_over_across(k).start()
+
+        either(k, before, tail)
 
     load_a(0, 0).start()
     load_g(0).start()
@@ -154,7 +202,7 @@
     pl.semaphore_wait(barrier, 3)
 
     def step(k, carry):
-        n, c, r = place(k)
+        n, c, r = place(dims, k)
 
         @pl.when(r == 0)
         def _():
@@ -228,10 +276,20 @@
     loop(since - since // GATHER_SKIP - FINISH_LAG, steps, finish)
 
     def drain(k):
-        gather_second(k).wait_send()
         gather_first(k).wait_send()
-        relay(k).wait_send()
-        hand_over(k).wait()
+
+        def before():
+            gather_second(k).wait_send()
+            relay(k).wait_send()
+            hand_over(k).wait()
+
+        def tail():
+            gather_later(k).wait_send()
+            hand_over_own(k).wait()
+            hand_over_later(k).wait()
+            hand_over_across(k).wait()
+
+        either(k, before, tail)
 
     loop(0, steps, drain)
     for k in range(steps - 2, steps):
@@ -240,6 +298,70 @@
         exchange_one(k).wait_send()
     for k in range(steps - RING_TWO, steps):
         exchange_two(k).wait_send()
+
+
+def copy_kernel(mats, d, src, dst, buffer, sem_in, sem_out):
+    blocks = [(n, r) for n in range(mats) for r in range(0, d, COPY_ROWS)]
+
+    def load(i):
+        n, r = blocks[i]
+        return pltpu.make_async_copy(src.at[n, pl.ds(r, COPY_ROWS)], buffer.at[i % COPY_SLOTS], sem_in.at[i % COPY_SLOTS])
+
+    def store(i):
+        n, r = blocks[i]
+        return pltpu.make_async_copy(buffer.at[i % COPY_SLOTS], dst.at[n, pl.ds(r, COPY_ROWS)], sem_out.at[i % COPY_SLOTS])
+
+    ahead = COPY_SLOTS // 2
+    for i in range(ahead):
+        load(i).start()
+    for i in range(len(blocks)):
+        load(i).wait()
+        store(i).start()
+        if i + ahead < len(blocks):
+            if i + ahead >= COPY_SLOTS:
+                store(i + ahead - COPY_SLOTS).wait()
+            load(i + ahead).start()
+    for i in range(len(blocks) - COPY_SLOTS, len(blocks)):
+        store(i).wait()
+
+
+def put_kernel(dims, starts, steps, *refs):
+    count = len(starts)
+    sources, dst, buffer, sem_in, sem_out = refs[:count], refs[count + 1], refs[-3], refs[-2], refs[-1]
+    eighth = ROWS // 8
+    rows = [start(lax.axis_index("dp")) for start in starts]
+
+    def load(i):
+        return pltpu.make_async_copy(sources[i], buffer.at[i], sem_in.at[i])
+
+    def store(i, j):
+        place = dst.at[index(dims, steps - AFTER + j, rows[i], eighth)]
+        return pltpu.make_async_copy(buffer.at[i, j], place, sem_out.at[i, j])
+
+    for i in range(count):
+        load(i).start()
+    for i in range(count):
+        load(i).wait()
+        for j in range(AFTER):
+            store(i, j).start()
+    for i in range(count):
+        for j in range(AFTER):
+            store(i, j).wait()
+
+
+def there_of(me):
+    core, first_bit, second_bit = position(me)
+    return core * (ROWS // 2) + first_bit * (ROWS // 4) + (1 - second_bit) * (ROWS // 8)
+
+
+def opposite_of(me):
+    core, first_bit, second_bit = position(me)
+    return core * (ROWS // 2) + (1 - first_bit) * (ROWS // 4) + (1 - second_bit) * (ROWS // 8)
+
+
+def mates_opposite_of(me):
+    core, first_bit, second_bit = position(me)
+    return (1 - core) * (ROWS // 2) + (1 - second_bit) * (ROWS // 4) + (1 - first_bit) * (ROWS // 8)
 
 
 def solution(mesh):
@@ -250,11 +372,14 @@
         half, quarter, eighth = ROWS // 2, ROWS // 4, ROWS // 8
         bf16, f32 = jnp.bfloat16, jnp.float32
         dma = pltpu.SemaphoreType.DMA
-        return pl.pallas_call(
-            functools.partial(kernel, (mats, tokens, d, ff)),
-            out_shape=jax.ShapeDtypeStruct((mats, d, ff), bf16),
+        dims = (mats, tokens, d, ff)
+        whole = jax.ShapeDtypeStruct((mats, d, ff), bf16)
+        hbm = pl.BlockSpec(memory_space=pl.ANY)
+        summed, later = pl.pallas_call(
+            functools.partial(kernel, dims),
+            out_shape=(whole, jax.ShapeDtypeStruct((AFTER, eighth, COLS), bf16)),
             in_specs=[pl.BlockSpec(memory_space=pl.ANY)] * 2,
-            out_specs=pl.BlockSpec(memory_space=pl.ANY),
+            out_specs=(hbm, hbm),
             scratch_shapes=[
                 pltpu.VMEM((2, tokens, d), bf16),
                 pltpu.VMEM((2, tokens, COLS), bf16),
@@ -277,11 +402,47 @@
                 dma((RING_TWO,)),
                 dma((RING_TWO,)),
             ]
-            + [dma((steps,))] * 9,
+            + [dma((steps,))] * 9
+            + [dma((AFTER,))] * 2,
             compiler_params=pltpu.CompilerParams(
                 collective_id=0, has_side_effects=True, vmem_limit_bytes=VMEM_LIMIT
             ),
         )(a, g)
+
+        opposite = lax.ppermute(later, "dp", [(i, i ^ (2 if i % 2 else 4)) for i in range(8)])
+        result = pl.pallas_call(
+            functools.partial(copy_kernel, mats, d),
+            out_shape=whole,
+            in_specs=[hbm],
+            out_specs=hbm,
+            scratch_shapes=[pltpu.VMEM((COPY_SLOTS, COPY_ROWS, ff), bf16), dma((COPY_SLOTS,)), dma((COPY_SLOTS,))],
+            compiler_params=pltpu.CompilerParams(vmem_limit_bytes=50 * 2**20),
+            cost_estimate=pl.CostEstimate(flops=2 * 10**9, bytes_accessed=4 * mats * d * ff, transcendentals=0),
+            name="copy",
+        )(summed)
+
+        def put(result, *sources_and_starts):
+            sources, starts = sources_and_starts[::2], sources_and_starts[1::2]
+            return pl.pallas_call(
+                functools.partial(put_kernel, dims, starts, steps),
+                out_shape=whole,
+                in_specs=[hbm] * (len(sources) + 1),
+                out_specs=hbm,
+                scratch_shapes=[
+                    pltpu.VMEM((len(sources), AFTER, eighth, COLS), bf16),
+                    dma((len(sources),)),
+                    dma((len(sources), AFTER)),
+                ],
+                input_output_aliases={len(sources): 0},
+                compiler_params=pltpu.CompilerParams(vmem_limit_bytes=16 * 2**20),
+                cost_estimate=pl.CostEstimate(flops=2 * 10**8, bytes_accessed=4 * len(sources) * later.size, transcendentals=0),
+                name="put",
+            )(*sources, result)
+
+        opposite, result = lax.optimization_barrier((opposite, result))
+        mates = lax.ppermute(opposite, "dp", [(i, i ^ 1) for i in range(8)])
+        result = put(result, later, there_of, opposite, opposite_of)
+        return put(result, mates, mates_opposite_of)
 
     return jax.shard_map(
         step,

time: 252 us -> 244 us (0.968)
  local copies, waits for them, and re-layouts: 18 us -> 0.01 us
  Pallas kernels: 234 us -> 241 us
    unnamed x1 -> x2, local copies, waits for them, and re-layouts: 18 us -> 0.01 us
    pallas_call x1 -> x4, Pallas kernels: 234 us -> 241 us  [the longest x1 218 us: step(): pl.pallas_call(functools.partial(kernel, dims), out_shape=(whole, jax.Sha...]
  transfers between devices with their start and end apart: 0 -> 2, of which waited for: 0 -> 2; matrix products, arithmetic and copies ran while one was open for 0% -> 0% of each run, Pallas kernels for 0% -> 9%
where the time goes in v3:
time: 244 us
  Pallas kernels  241 us (99%)
    pallas_call x1, Pallas kernels, step(): pl.pallas_call(functools.partial(kernel, dims), out_shape=(whole, jax.Sha...  218 us
    pallas_call x1, Pallas kernels, step(): pl.pallas_call(functools.partial(copy_kernel, mats, d), out_shape=whole,...  18.7 us
  transfers between devices with their start and end apart: 2, of which 2 were waited for; matrix products, arithmetic and copies ran while one was open for 0% of the time, Pallas kernels for 9%

profile of v3, /device:TPU:0, one launch (start us, length us, event | category | flops | bytes accessed | tf_op | source)
XLA Modules:
  0.0 244.3 jit_solution(7090813524428695570)
XLA Ops:
  0.0 218.2 %shard_map.28 = (bf16[4,1024,3200]{2,1,0:T(8,128)(2,1)}, bf16[20,64,640]{2,1,0:T(8,128)(2,1)}) custom-call(bf16[1,4,4096,1024]{3,2,1,0:T(8,128)(2,1)} %a.1, bf16[1,4,4096,3200]{3,2,1,0:T(8,128)(2,1)} %g.1), custom_call_target="tpu_custom_call" | custom-call | tf_op jit(solution)/shard_map/pallas_call | solution.py:378
  218.2 1.5 collective-permute-start
  219.7 0.0 copy-start
  219.7 18.7 %copy.8.refs_2_ = bf16[4,1024,3200]{2,1,0:T(8,128)(2,1)} custom-call(bf16[4,1024,3200]{2,1,0:T(8,128)(2,1)} %get-tuple-element.10.src), custom_call_target="tpu_custom_call" | custom-call | flops 2000000000 | bytes 52428800 | tf_op jit(solution)/shard_map/copy/pallas_call | solution.py:413
  238.3 1.0 collective-permute-done.refs_1_
  239.3 0.0 collective-permute-start.1
  239.3 0.0 copy-done
  239.3 2.4 put.2.refs_1_
  241.8 1.1 collective-permute-done.1.refs_0_
  242.8 1.5 put.3
Async XLA Ops:
  218.2 21.1 %collective-permute-start = (bf16[20,64,640]{2,1,0:T(8,128)(2,1)}, bf16[20,64,640]{2,1,0:T(8,128)(2,1)S(1)}, u32[]{:S(2)}, u32[]{:S(2)}) collective-permute-start(bf16[20,64,640]{2,1,0:T(8,128)(2,1)} %get-tuple-element.9.refs_0_), channel_id=1, source_target_pairs={{0,4},{1,3},{2,6},{3,1},{4,0},{5,7},{6,2},{7,5}} | collective-permute-start | bytes 4915208 | tf_op jit(solution)/shard_map/ppermute | solution.py:412
  219.7 19.7 %copy-start = (bf16[20,64,640]{2,1,0:T(8,128)(2,1)S(1)}, bf16[20,64,640]{2,1,0:T(8,128)(2,1)}, u32[]{:S(2)}) copy-start(bf16[20,64,640]{2,1,0:T(8,128)(2,1)} %get-tuple-element.9.refs_0_) | copy-start | bytes 4915204
  239.3 3.5 %collective-permute-start.1 = (bf16[20,64,640]{2,1,0:T(8,128)(2,1)S(1)}, bf16[20,64,640]{2,1,0:T(8,128)(2,1)S(1)}, u32[]{:S(2)}, u32[]{:S(2)}) collective-permute-start(bf16[20,64,640]{2,1,0:T(8,128)(2,1)S(1)} %collective-permute-done.refs_1_), channel_id=1, source_target_pairs={{0,1},{1,0},{2,3},{3,2},{4,5},{5,4},{6,7},{7,6}} | collective-permute-start | bytes 4915208 | tf_op jit(solution)/shard_map/ppermute | solution.py:443

commit v4 on v3

--- a/solution.py
+++ b/solution.py
@@ -13,10 +13,11 @@
 LAG_ONE, LAG_TWO = 2, 4
 RING_ONE, RING_TWO = 2 * LAG_ONE + 2, 2 * (LAG_TWO - LAG_ONE) + 2
 OWN_ONE, OWN_TWO = LAG_ONE + 1, LAG_TWO - LAG_ONE + 1
-GATHER_FROM, GATHER_SKIP = LAG_TWO, 6
-PASS_LAG, FINISH_LAG = 2, 4
-AFTER = 20
-COPY_ROWS, COPY_SLOTS = 256, 6
+SHORT_UNTIL = 5
+GATHER_SKIP = 8
+PIECES = 4
+PASS_LAG, FINISH_LAG, DRAIN_LAG = 2, 4, 8
+COPY_SLOTS = 16
 
 TAIL = 2
 
@@ -40,12 +41,12 @@
 
 def kernel(dims, a, g, out, later, a_v, g_v, half_send, half_own, half_recv, one_send, one_own, one_recv, two_send, two_own,
            two_recv, final, sem_a, sem_g, sem_hs, sem_hr, sem_1s, sem_1r, sem_2s, sem_2r, sem_fin, sem_3s, sem_3r,
-           sem_4s, sem_4r, sem_5s, sem_5r, sem_6s, sem_6r, sem_7s, sem_7r):
+           sem_4s, sem_4r, sem_5s, sem_5r, sem_6s, sem_6r, sem_7s, sem_7r,
+           sem_first):
     mats, tokens, d, ff = dims
     row_blocks, col_blocks = d // ROWS, ff // COLS
     steps = mats * row_blocks * col_blocks
     half, quarter, eighth = ROWS // 2, ROWS // 4, ROWS // 8
-    after = steps - AFTER
 
     me = lax.axis_index("dp")
     core, first_bit, second_bit = position(me)
@@ -69,8 +70,16 @@
         cols = pl.ds(pl.multiple_of(c * COLS, 128), COLS)
         return pltpu.make_async_copy(g.at[0, n, :, cols], g_v.at[i % 2], sem_g.at[i % 2])
 
+    def load_first(i):
+        size = tokens // PIECES
+        piece = pl.ds(i * size, size)
+        return (
+            pltpu.make_async_copy(a.at[0, 0, piece, pl.ds(0, ROWS)], a_v.at[0, piece, pl.ds(0, ROWS)], sem_first.at[0, i]),
+            pltpu.make_async_copy(g.at[0, 0, piece, pl.ds(0, COLS)], g_v.at[0, piece], sem_first.at[1, i]),
+        )
+
     def rows_of(k, start, size):
-        return out.at[index(dims, k, start, size)]
+        return out.at[k, pl.ds(pl.multiple_of(start, eighth), size)]
 
     own_half = core * half
     here = own_half + first_bit * quarter + second_bit * eighth
@@ -93,7 +102,7 @@
         return send(final.at[k], rows_of(k, here, eighth), sem_3s.at[k], sem_3r.at[k], second)
 
     def gather_later(k):
-        return send(final.at[k], later.at[k - after], sem_3s.at[k], sem_3r.at[k], second)
+        return send(final.at[k], later.at[k // 2], sem_3s.at[k], sem_3r.at[k], second)
 
     def gather_first(k):
         return send(final.at[k], rows_of(k, here, eighth), sem_4s.at[k], sem_4r.at[k], first)
@@ -108,10 +117,10 @@
         return send(final.at[k], rows_of(k, here, eighth), sem_6s.at[k], sem_6r.at[k], mate)
 
     def hand_over_later(k):
-        return send(later.at[k - after], rows_of(k, there, eighth), sem_5s.at[k], sem_5r.at[k], mate)
+        return send(later.at[k // 2], rows_of(k, there, eighth), sem_5s.at[k], sem_5r.at[k], mate)
 
     def hand_over_across(k):
-        return send(rows_of(k, across, eighth), rows_of(k, across, eighth), sem_7s.at[k - after], sem_7r.at[k - after], mate)
+        return send(rows_of(k, across, eighth), rows_of(k, across, eighth), sem_7s.at[k // 2], sem_7r.at[k // 2], mate)
 
     def product(k, start):
         n, c, r = place(dims, k)
@@ -157,8 +166,8 @@
         keep(k).start()
 
     def either(k, before, tail):
-        pl.when(k < after)(before)
-        pl.when(k >= after)(tail)
+        pl.when(k % 2 == 0)(before)
+        pl.when(k % 2 == 1)(tail)
 
     def gather(k):
         def before():
@@ -195,10 +204,42 @@
 
         either(k, before, tail)
 
-    load_a(0, 0).start()
-    load_g(0).start()
-    for r in range(1, row_blocks):
-        load_a(0, r).start()
+    def drain(k):
+        gather_first(k).wait_send()
+
+        def before():
+            gather_second(k).wait_send()
+            relay(k).wait_send()
+            hand_over(k).wait()
+
+        def tail():
+            gather_later(k).wait_send()
+            hand_over_own(k).wait()
+            hand_over_later(k).wait()
+            hand_over_across(k).wait()
+
+        either(k, before, tail)
+
+    for i in range(PIECES):
+        for copy in load_first(i):
+            copy.start()
+    mates_cols = pl.ds(pl.multiple_of((1 - core) * half, half), half)
+    for i in range(PIECES):
+        for copy in load_first(i):
+            copy.wait()
+        if i == PIECES - 1:
+            for r in range(1, row_blocks):
+                load_a(0, r).start()
+        piece = pl.ds(i * (tokens // PIECES), tokens // PIECES)
+        one = lax.dot_general(
+            a_v[0, piece, mates_cols], g_v[0, piece], (((0,), (0,)), ((), ())), preferred_element_type=jnp.float32
+        )
+        if i == 0:
+            half_own[0] = one
+        elif i < PIECES - 1:
+            half_own[0] += one
+        else:
+            half_send[0] = (half_own[0] + one).astype(jnp.bfloat16)
     pl.semaphore_wait(barrier, 3)
 
     def step(k, carry):
@@ -206,7 +247,9 @@
 
         @pl.when(r == 0)
         def _():
-            load_g(k // row_blocks).wait()
+            @pl.when(k > 0)
+            def _():
+                load_g(k // row_blocks).wait()
 
             @pl.when(k + row_blocks < steps)
             def _():
@@ -214,7 +257,9 @@
 
         @pl.when(c == 0)
         def _():
-            load_a(n, r).wait()
+            @pl.when(k > 0)
+            def _():
+                load_a(n, r).wait()
 
             @pl.when(n + 1 < mats)
             def _():
@@ -224,24 +269,31 @@
         def _():
             swap(k - 2).wait_send()
 
-        half_send[k % 2] = product(k, (1 - core) * half).astype(jnp.bfloat16)
+        @pl.when(k > 0)
+        def _():
+            half_send[k % 2] = product(k, (1 - core) * half).astype(jnp.bfloat16)
+
         swap(k).start()
         half_own[k % 2] = product(k, own_half)
         reduce_cores(k)
 
-        @pl.when(k >= LAG_ONE)
-        def _():
-            reduce_first(k - LAG_ONE)
-
-        @pl.when(k >= LAG_TWO)
-        def _():
-            reduce_second(k - LAG_TWO)
-
-        since = k - GATHER_FROM
-
-        @pl.when((since >= 0) & (since % GATHER_SKIP != GATHER_SKIP - 1))
-        def _():
-            i = since - since // GATHER_SKIP
+        more = jnp.minimum(k // SHORT_UNTIL, 1)
+
+        @pl.when((k >= 1) & (k != SHORT_UNTIL))
+        def _():
+            reduce_first(k - 1 - (LAG_ONE - 1) * more)
+
+        @pl.when((k >= 2) & (k != SHORT_UNTIL) & (k != SHORT_UNTIL + 1))
+        def _():
+            reduce_second(k - 2 - (LAG_TWO - 2) * more)
+
+        since = k - SHORT_UNTIL - LAG_TWO + 2
+        skipped = more * (LAG_TWO - 2 + since // GATHER_SKIP)
+        now = (k < SHORT_UNTIL) | ((since >= 0) & (since % GATHER_SKIP != GATHER_SKIP - 1))
+
+        @pl.when((k >= 2) & now)
+        def _():
+            i = k - 2 - skipped
             gather(i)
 
             @pl.when(i >= PASS_LAG)
@@ -252,11 +304,15 @@
             def _():
                 finish(i - FINISH_LAG)
 
+            @pl.when(i >= DRAIN_LAG)
+            def _():
+                drain(i - DRAIN_LAG)
+
         return carry
 
     lax.fori_loop(0, steps, step, 0)
-    since = steps - GATHER_FROM
-    started = since - since // GATHER_SKIP
+    started = steps - LAG_TWO - (steps - SHORT_UNTIL - LAG_TWO + 2) // GATHER_SKIP
+    passed, finished, drained = started - PASS_LAG, started - FINISH_LAG, started - DRAIN_LAG
 
     def loop(low, high, f):
         def body(k, carry):
@@ -272,26 +328,14 @@
         ready = min(started + TAIL, k - LAG_TWO + 1) if k + 1 < steps + LAG_TWO else steps
         loop(started, ready, gather)
         started = max(started, ready)
-    loop(since - since // GATHER_SKIP - PASS_LAG, steps, pass_on)
-    loop(since - since // GATHER_SKIP - FINISH_LAG, steps, finish)
-
-    def drain(k):
-        gather_first(k).wait_send()
-
-        def before():
-            gather_second(k).wait_send()
-            relay(k).wait_send()
-            hand_over(k).wait()
-
-        def tail():
-            gather_later(k).wait_send()
-            hand_over_own(k).wait()
-            hand_over_later(k).wait()
-            hand_over_across(k).wait()
-
-        either(k, before, tail)
-
-    loop(0, steps, drain)
+    loop(passed, steps, pass_on)
+
+    def finish_and_drain(k):
+        finish(k)
+        drain(k - DRAIN_LAG + FINISH_LAG)
+
+    loop(finished, steps, finish_and_drain)
+    loop(steps - DRAIN_LAG + FINISH_LAG, steps, drain)
     for k in range(steps - 2, steps):
         swap(k).wait_send()
     for k in range(steps - RING_ONE, steps):
@@ -300,52 +344,44 @@
         exchange_two(k).wait_send()
 
 
-def copy_kernel(mats, d, src, dst, buffer, sem_in, sem_out):
-    blocks = [(n, r) for n in range(mats) for r in range(0, d, COPY_ROWS)]
+def copy_kernel(dims, src, dst, buffer, sem_in, sem_out):
+    steps = src.shape[0]
 
     def load(i):
-        n, r = blocks[i]
-        return pltpu.make_async_copy(src.at[n, pl.ds(r, COPY_ROWS)], buffer.at[i % COPY_SLOTS], sem_in.at[i % COPY_SLOTS])
+        return pltpu.make_async_copy(src.at[i], buffer.at[i % COPY_SLOTS], sem_in.at[i % COPY_SLOTS])
 
     def store(i):
-        n, r = blocks[i]
-        return pltpu.make_async_copy(buffer.at[i % COPY_SLOTS], dst.at[n, pl.ds(r, COPY_ROWS)], sem_out.at[i % COPY_SLOTS])
+        return pltpu.make_async_copy(
+            buffer.at[i % COPY_SLOTS], dst.at[index(dims, i, 0, ROWS)], sem_out.at[i % COPY_SLOTS]
+        )
 
     ahead = COPY_SLOTS // 2
     for i in range(ahead):
         load(i).start()
-    for i in range(len(blocks)):
+    for i in range(steps):
         load(i).wait()
         store(i).start()
-        if i + ahead < len(blocks):
+        if i + ahead < steps:
             if i + ahead >= COPY_SLOTS:
                 store(i + ahead - COPY_SLOTS).wait()
             load(i + ahead).start()
-    for i in range(len(blocks) - COPY_SLOTS, len(blocks)):
+    for i in range(steps - COPY_SLOTS, steps):
         store(i).wait()
 
 
-def put_kernel(dims, starts, steps, *refs):
+def put_kernel(dims, starts, *refs):
     count = len(starts)
-    sources, dst, buffer, sem_in, sem_out = refs[:count], refs[count + 1], refs[-3], refs[-2], refs[-1]
-    eighth = ROWS // 8
+    sources, dst, sem = refs[:count], refs[count + 1], refs[-1]
     rows = [start(lax.axis_index("dp")) for start in starts]
 
-    def load(i):
-        return pltpu.make_async_copy(sources[i], buffer.at[i], sem_in.at[i])
-
     def store(i, j):
-        place = dst.at[index(dims, steps - AFTER + j, rows[i], eighth)]
-        return pltpu.make_async_copy(buffer.at[i, j], place, sem_out.at[i, j])
+        return pltpu.make_async_copy(sources[i].at[j], dst.at[index(dims, 2 * j + 1, rows[i], ROWS // 8)], sem.at[i, j])
 
     for i in range(count):
-        load(i).start()
-    for i in range(count):
-        load(i).wait()
-        for j in range(AFTER):
+        for j in range(sources[i].shape[0]):
             store(i, j).start()
     for i in range(count):
-        for j in range(AFTER):
+        for j in range(sources[i].shape[0]):
             store(i, j).wait()
 
 
@@ -377,7 +413,7 @@
         hbm = pl.BlockSpec(memory_space=pl.ANY)
         summed, later = pl.pallas_call(
             functools.partial(kernel, dims),
-            out_shape=(whole, jax.ShapeDtypeStruct((AFTER, eighth, COLS), bf16)),
+            out_shape=(jax.ShapeDtypeStruct((steps, ROWS, COLS), bf16), jax.ShapeDtypeStruct((steps // 2, eighth, COLS), bf16)),
             in_specs=[pl.BlockSpec(memory_space=pl.ANY)] * 2,
             out_specs=(hbm, hbm),
             scratch_shapes=[
@@ -403,7 +439,8 @@
                 dma((RING_TWO,)),
             ]
             + [dma((steps,))] * 9
-            + [dma((AFTER,))] * 2,
+            + [dma((steps // 2,))] * 2
+            + [dma((2, PIECES))],
             compiler_params=pltpu.CompilerParams(
                 collective_id=0, has_side_effects=True, vmem_limit_bytes=VMEM_LIMIT
             ),
@@ -411,11 +448,11 @@
 
         opposite = lax.ppermute(later, "dp", [(i, i ^ (2 if i % 2 else 4)) for i in range(8)])
         result = pl.pallas_call(
-            functools.partial(copy_kernel, mats, d),
+            functools.partial(copy_kernel, dims),
             out_shape=whole,
             in_specs=[hbm],
             out_specs=hbm,
-            scratch_shapes=[pltpu.VMEM((COPY_SLOTS, COPY_ROWS, ff), bf16), dma((COPY_SLOTS,)), dma((COPY_SLOTS,))],
+            scratch_shapes=[pltpu.VMEM((COPY_SLOTS, ROWS, COLS), bf16), dma((COPY_SLOTS,)), dma((COPY_SLOTS,))],
             compiler_params=pltpu.CompilerParams(vmem_limit_bytes=50 * 2**20),
             cost_estimate=pl.CostEstimate(flops=2 * 10**9, bytes_accessed=4 * mats * d * ff, transcendentals=0),
             name="copy",
@@ -424,15 +461,11 @@
         def put(result, *sources_and_starts):
             sources, starts = sources_and_starts[::2], sources_and_starts[1::2]
             return pl.pallas_call(
-                functools.partial(put_kernel, dims, starts, steps),
+                functools.partial(put_kernel, dims, starts),
                 out_shape=whole,
                 in_specs=[hbm] * (len(sources) + 1),
                 out_specs=hbm,
-                scratch_shapes=[
-                    pltpu.VMEM((len(sources), AFTER, eighth, COLS), bf16),
-                    dma((len(sources),)),
-                    dma((len(sources), AFTER)),
-                ],
+                scratch_shapes=[dma((len(sources), steps // 2))],
                 input_output_aliases={len(sources): 0},
                 compiler_params=pltpu.CompilerParams(vmem_limit_bytes=16 * 2**20),
                 cost_estimate=pl.CostEstimate(flops=2 * 10**8, bytes_accessed=4 * len(sources) * later.size, transcendentals=0),

time: 244 us -> 242 us (level)
  Pallas kernels: 241 us -> 238 us
    pallas_call x4, Pallas kernels: 241 us -> 238 us  [the longest x1 216 us: step(): pl.pallas_call(functools.partial(kernel, dims), out_shape=(jax.ShapeDtype...]
  transfers between devices with their start and end apart: 2 -> 2, of which waited for: 2 -> 2; matrix products, arithmetic and copies ran while one was open for 0% -> 0% of each run, Pallas kernels for 9% -> 8%
where the time goes in v4:
time: 242 us
  Pallas kernels  238 us (98%)
  waiting for transfers between devices  3.18 us (1%)
    pallas_call x1, Pallas kernels, step(): pl.pallas_call(functools.partial(kernel, dims), out_shape=(jax.ShapeDtype...  216 us
    pallas_call x1, Pallas kernels, step(): pl.pallas_call(functools.partial(copy_kernel, dims), out_shape=whole, in_...  18.4 us
  transfers between devices with their start and end apart: 2, of which 2 were waited for; matrix products, arithmetic and copies ran while one was open for 0% of the time, Pallas kernels for 8%

profile of v4, /device:TPU:0, one launch (start us, length us, event | category | flops | bytes accessed | tf_op | source)
XLA Modules:
  0.0 242.3 jit_solution(3291107603825512735)
XLA Ops:
  0.0 216.4 %shard_map.28 = (bf16[40,512,640]{2,1,0:T(8,128)(2,1)}, bf16[20,64,640]{2,1,0:T(8,128)(2,1)}) custom-call(bf16[1,4,4096,1024]{3,2,1,0:T(8,128)(2,1)} %a.1, bf16[1,4,4096,3200]{3,2,1,0:T(8,128)(2,1)} %g.1), custom_call_target="tpu_custom_call" | custom-call | tf_op jit(solution)/shard_map/pallas_call | solution.py:414
  216.4 1.0 collective-permute-start
  217.4 0.0 copy-start
  217.4 18.4 %copy.8.refs_2_ = bf16[4,1024,3200]{2,1,0:T(8,128)(2,1)} custom-call(bf16[40,512,640]{2,1,0:T(8,128)(2,1)} %get-tuple-element.10.src), custom_call_target="tpu_custom_call" | custom-call | flops 2000000000 | bytes 52428800 | tf_op jit(solution)/shard_map/copy/pallas_call | solution.py:450
  235.8 1.7 collective-permute-done.refs_1_
  237.5 0.0 collective-permute-start.1
  237.5 0.0 copy-done
  237.5 2.0 put.2.refs_1_
  239.6 1.5 collective-permute-done.1.refs_0_
  241.0 1.3 put.3
Async XLA Ops:
  216.4 21.1 %collective-permute-start = (bf16[20,64,640]{2,1,0:T(8,128)(2,1)}, bf16[20,64,640]{2,1,0:T(8,128)(2,1)S(1)}, u32[]{:S(2)}, u32[]{:S(2)}) collective-permute-start(bf16[20,64,640]{2,1,0:T(8,128)(2,1)} %get-tuple-element.9.refs_0_), channel_id=1, source_target_pairs={{0,4},{1,3},{2,6},{3,1},{4,0},{5,7},{6,2},{7,5}} | collective-permute-start | bytes 4915208 | tf_op jit(solution)/shard_map/ppermute | solution.py:449
  217.4 20.1 %copy-start = (bf16[20,64,640]{2,1,0:T(8,128)(2,1)S(1)}, bf16[20,64,640]{2,1,0:T(8,128)(2,1)}, u32[]{:S(2)}) copy-start(bf16[20,64,640]{2,1,0:T(8,128)(2,1)} %get-tuple-element.9.refs_0_) | copy-start | bytes 4915204
  237.5 3.5 %collective-permute-start.1 = (bf16[20,64,640]{2,1,0:T(8,128)(2,1)S(1)}, bf16[20,64,640]{2,1,0:T(8,128)(2,1)S(1)}, u32[]{:S(2)}, u32[]{:S(2)}) collective-permute-start(bf16[20,64,640]{2,1,0:T(8,128)(2,1)S(1)} %collective-permute-done.refs_1_), channel_id=1, source_target_pairs={{0,1},{1,0},{2,3},{3,2},{4,5},{5,4},{6,7},{7,6}} | collective-permute-start | bytes 4915208 | tf_op jit(solution)/shard_map/ppermute | solution.py:476

commit v5 on v4

--- a/solution.py
+++ b/solution.py
@@ -70,11 +70,17 @@
         cols = pl.ds(pl.multiple_of(c * COLS, 128), COLS)
         return pltpu.make_async_copy(g.at[0, n, :, cols], g_v.at[i % 2], sem_g.at[i % 2])
 
+    mates_cols = pl.ds(pl.multiple_of((1 - core) * half, half), half)
+    own_cols = pl.ds(pl.multiple_of(core * half, half), half)
+
+    def load_own():
+        return pltpu.make_async_copy(a.at[0, 0, :, own_cols], a_v.at[0, :, own_cols], sem_a.at[0, 0])
+
     def load_first(i):
         size = tokens // PIECES
         piece = pl.ds(i * size, size)
         return (
-            pltpu.make_async_copy(a.at[0, 0, piece, pl.ds(0, ROWS)], a_v.at[0, piece, pl.ds(0, ROWS)], sem_first.at[0, i]),
+            pltpu.make_async_copy(a.at[0, 0, piece, mates_cols], a_v.at[0, piece, mates_cols], sem_first.at[0, i]),
             pltpu.make_async_copy(g.at[0, 0, piece, pl.ds(0, COLS)], g_v.at[0, piece], sem_first.at[1, i]),
         )
 
@@ -223,7 +229,7 @@
     for i in range(PIECES):
         for copy in load_first(i):
             copy.start()
-    mates_cols = pl.ds(pl.multiple_of((1 - core) * half, half), half)
+    load_own().start()
     for i in range(PIECES):
         for copy in load_first(i):
             copy.wait()
@@ -240,6 +246,7 @@
             half_own[0] += one
         else:
             half_send[0] = (half_own[0] + one).astype(jnp.bfloat16)
+    load_own().wait()
     pl.semaphore_wait(barrier, 3)
 
     def step(k, carry):
@@ -328,12 +335,11 @@
         ready = min(started + TAIL, k - LAG_TWO + 1) if k + 1 < steps + LAG_TWO else steps
         loop(started, ready, gather)
         started = max(started, ready)
-    loop(passed, steps, pass_on)
-
     def finish_and_drain(k):
         finish(k)
         drain(k - DRAIN_LAG + FINISH_LAG)
 
+    loop(passed, steps, pass_on)
     loop(finished, steps, finish_and_drain)
     loop(steps - DRAIN_LAG + FINISH_LAG, steps, drain)
     for k in range(steps - 2, steps):

time: 242 us -> 242 us (level)
  no operation moved by 1% of the time
where the time goes in v5:
time: 242 us
  Pallas kernels  238 us (98%)
  waiting for transfers between devices  3.29 us (1%)
    pallas_call x1, Pallas kernels, step(): pl.pallas_call(functools.partial(kernel, dims), out_shape=(jax.ShapeDtype...  216 us
    pallas_call x1, Pallas kernels, step(): pl.pallas_call(functools.partial(copy_kernel, dims), out_shape=whole, in_...  18.4 us
  transfers between devices with their start and end apart: 2, of which 2 were waited for; matrix products, arithmetic and copies ran while one was open for 0% of the time, Pallas kernels for 8%

profile of v5, /device:TPU:0, one launch (start us, length us, event | category | flops | bytes accessed | tf_op | source)
XLA Modules:
  0.0 241.9 jit_solution(3543480952800245171)
XLA Ops:
  0.0 215.9 %shard_map.28 = (bf16[40,512,640]{2,1,0:T(8,128)(2,1)}, bf16[20,64,640]{2,1,0:T(8,128)(2,1)}) custom-call(bf16[1,4,4096,1024]{3,2,1,0:T(8,128)(2,1)} %a.1, bf16[1,4,4096,3200]{3,2,1,0:T(8,128)(2,1)} %g.1), custom_call_target="tpu_custom_call" | custom-call | tf_op jit(solution)/shard_map/pallas_call | solution.py:420
  215.9 0.9 collective-permute-start
  216.8 0.0 copy-start
  216.8 18.4 %copy.8.refs_2_ = bf16[4,1024,3200]{2,1,0:T(8,128)(2,1)} custom-call(bf16[40,512,640]{2,1,0:T(8,128)(2,1)} %get-tuple-element.10.src), custom_call_target="tpu_custom_call" | custom-call | flops 2000000000 | bytes 52428800 | tf_op jit(solution)/shard_map/copy/pallas_call | solution.py:456
  235.2 1.8 collective-permute-done.refs_1_
  237.1 0.0 collective-permute-start.1
  237.1 0.0 copy-done
  237.1 2.0 put.2.refs_1_
  239.1 1.5 collective-permute-done.1.refs_0_
  240.6 1.3 put.3
Async XLA Ops:
  215.9 21.1 %collective-permute-start = (bf16[20,64,640]{2,1,0:T(8,128)(2,1)}, bf16[20,64,640]{2,1,0:T(8,128)(2,1)S(1)}, u32[]{:S(2)}, u32[]{:S(2)}) collective-permute-start(bf16[20,64,640]{2,1,0:T(8,128)(2,1)} %get-tuple-element.9.refs_0_), channel_id=1, source_target_pairs={{0,4},{1,3},{2,6},{3,1},{4,0},{5,7},{6,2},{7,5}} | collective-permute-start | bytes 4915208 | tf_op jit(solution)/shard_map/ppermute | solution.py:455
  216.8 20.2 %copy-start = (bf16[20,64,640]{2,1,0:T(8,128)(2,1)S(1)}, bf16[20,64,640]{2,1,0:T(8,128)(2,1)}, u32[]{:S(2)}) copy-start(bf16[20,64,640]{2,1,0:T(8,128)(2,1)} %get-tuple-element.9.refs_0_) | copy-start | bytes 4915204
  237.1 3.5 %collective-permute-start.1 = (bf16[20,64,640]{2,1,0:T(8,128)(2,1)S(1)}, bf16[20,64,640]{2,1,0:T(8,128)(2,1)S(1)}, u32[]{:S(2)}, u32[]{:S(2)}) collective-permute-start(bf16[20,64,640]{2,1,0:T(8,128)(2,1)S(1)} %collective-permute-done.refs_1_), channel_id=1, source_target_pairs={{0,1},{1,0},{2,3},{3,2},{4,5},{5,4},{6,7},{7,6}} | collective-permute-start | bytes 4915208 | tf_op jit(solution)/shard_map/ppermute | solution.py:482
